TPU v7x, 32 devices: a whole 2x2x4 slice. The times are simulated.
32 devices in a mesh: node: 8 (over z, y), dev: 4 (over x, core).
Axes of the slice: x: 2, y: 2, z: 4, core: 2. Of those that a mesh axis runs over, the one named last changes fastest.
Arguments:
- tokens: bfloat16 [128, 5120], P(('node', 'dev')), may hold values from -6 to 6
- node_pick: int32 [128, 3], P(('node', 'dev')), may hold values from 0 to 7, as said below
- expert_pick: int32 [128, 6], P(('node', 'dev')), may hold values from 0 to 3, as said below
- gate_weight: bfloat16 [128, 6], P(('node', 'dev')), may hold values from 0.099609375 to 1
- w_gate: bfloat16 [24576, 5120], P(('node', 'dev')), may hold values from -0.078125 to 0.078125
- w_up: bfloat16 [24576, 5120], P(('node', 'dev')), may hold values from -0.078125 to 0.078125
- w_down: bfloat16 [24576, 5120], P(('node', 'dev')), may hold values from -0.21875 to 0.21875
Outputs:
- mixed_out: bfloat16 [128, 5120], P(('node', 'dev'))
Inputs may be any that keep to these rules, and one draw needn't show every extreme that they name: `node_pick`: A token's three nodes differ. On every device at most 2 of its 4 tokens choose one node, and some node is chosen by exactly 2 of them. `expert_pick`: columns 2k and 2k + 1 name two different experts of node node_pick[t, k]. Among the tokens of all devices with one index along dev, at most 12 of those choosing one node pick one same expert of it; this is reached somewhere in every draw.
All inputs are finite; a program needn't handle non-finite values.
Results may differ from a plain program's by a relative error of at most 0.009.
Values may be sent and summed in bfloat16 or wider, within the bound.
A program may use at most 64 MiB of HBM per device.

v0:
```python
import jax
import jax.numpy as jnp
from jax import lax
from jax.sharding import PartitionSpec as P

EXP_NODE = 4


def on_device(tokens, node_pick, expert_pick, gate_weight, w_gate, w_up, w_down):
    node_count = lax.axis_size("node")
    dev_count = lax.axis_size("dev")
    tok_rows = tokens.shape[0]
    feature_dim = tokens.shape[1]
    slot_count = 3 * tok_rows
    cycle_len = min(node_count, max(3, slot_count // 2))
    node_cap = (slot_count + cycle_len - 1) // cycle_len
    slices = dev_count // EXP_NODE
    node_slots = node_count * node_cap
    dest_node = node_pick.reshape(slot_count)
    slot_order = jnp.arange(slot_count, dtype=jnp.int32)
    earlier = (dest_node[:, None] == dest_node[None, :]) & (
        slot_order[None, :] < slot_order[:, None]
    )
    slot_rank = jnp.sum(earlier.astype(jnp.int32), axis=1)
    position = dest_node * node_cap + slot_rank
    place_table = (jnp.arange(node_slots, dtype=jnp.int32)[:, None] == position[None, :]).astype(
        jnp.bfloat16
    )
    local_pick = expert_pick.reshape(tok_rows, 3, 2)
    weights = gate_weight.reshape(tok_rows, 3, 2).astype(jnp.float32)
    chosen = (local_pick[..., None] == jnp.arange(EXP_NODE, dtype=jnp.int32)).astype(jnp.float32)
    slot_meta = (
        jnp.sum(weights[..., None] * chosen, axis=2)
        .reshape(slot_count, EXP_NODE)
        .astype(jnp.bfloat16)
    )
    sent_rows = jnp.dot(
        place_table, jnp.repeat(tokens, 3, axis=0), preferred_element_type=jnp.float32
    )
    sent_meta = jnp.dot(place_table, slot_meta, preferred_element_type=jnp.float32)
    sent_rows = sent_rows.astype(jnp.bfloat16).reshape(node_count, node_cap, feature_dim)
    sent_meta = sent_meta.astype(jnp.bfloat16).reshape(node_count, node_cap, EXP_NODE)
    got_rows, got_meta = (
        lax.all_to_all(sent_rows, "node", split_axis=0, concat_axis=0, tiled=True),
        lax.all_to_all(sent_meta, "node", split_axis=0, concat_axis=0, tiled=True),
    )
    got_rows = got_rows.reshape(node_slots, feature_dim)
    got_meta = got_meta.reshape(node_slots, EXP_NODE)
    is_live = got_meta > 0
    live_rank = jnp.cumsum(is_live.astype(jnp.int32), axis=0) - 1
    cap_ids = jnp.arange(slot_count, dtype=jnp.int32)[None, :, None]
    pick_table = is_live.T[:, None, :] & (live_rank.T[:, None, :] == cap_ids)
    pick_table = pick_table.reshape(EXP_NODE * slot_count, node_slots)
    packed = jnp.dot(
        pick_table.astype(jnp.bfloat16), got_rows, preferred_element_type=jnp.float32
    ).astype(jnp.bfloat16)
    outgoing = jnp.broadcast_to(
        packed.reshape(EXP_NODE, 1, slot_count, feature_dim),
        (EXP_NODE, slices, slot_count, feature_dim),
    ).reshape(dev_count, slot_count, feature_dim)
    arrived = lax.all_to_all(outgoing, "dev", split_axis=0, concat_axis=0, tiled=True)
    item_count = arrived.shape[1]
    flat_rows = arrived.reshape(dev_count * item_count, feature_dim)
    dims = (((1,), (1,)), ((), ()))
    gate_act = lax.dot_general(flat_rows, w_gate, dims, preferred_element_type=jnp.float32)
    up_act = lax.dot_general(flat_rows, w_up, dims, preferred_element_type=jnp.float32)
    hidden = (jax.nn.silu(gate_act) * up_act).astype(jnp.bfloat16)
    partial_value = jnp.dot(hidden, w_down, preferred_element_type=jnp.float32).astype(jnp.bfloat16)
    partial_value = partial_value.reshape(dev_count, item_count, feature_dim)
    returned = lax.all_to_all(partial_value, "dev", split_axis=0, concat_axis=0, tiled=True)
    expert_out = jnp.sum(
        returned.astype(jnp.float32).reshape(EXP_NODE, slices, slot_count, feature_dim), axis=1
    )
    expert_out = expert_out.reshape(EXP_NODE * slot_count, feature_dim)
    combine = pick_table.T.astype(jnp.float32) * jnp.repeat(
        got_meta.astype(jnp.float32), slot_count, axis=1
    )
    node_out = jnp.dot(
        combine, expert_out, precision=lax.Precision.HIGHEST, preferred_element_type=jnp.float32
    )
    node_out = node_out.astype(jnp.bfloat16).reshape(node_count, node_cap, feature_dim)
    home_rows = lax.all_to_all(node_out, "node", split_axis=0, concat_axis=0, tiled=True).reshape(
        node_slots, feature_dim
    )
    per_slot = jnp.dot(place_table.T, home_rows, preferred_element_type=jnp.float32)
    return jnp.sum(per_slot.reshape(tok_rows, 3, feature_dim), axis=1).astype(jnp.bfloat16)


def solution(mesh):
    in_specs = (
        P(("node", "dev"), None),
        P(("node", "dev"), None),
        P(("node", "dev"), None),
        P(("node", "dev"), None),
        P(("node", "dev"), None),
        P(("node", "dev"), None),
        P(("node", "dev"), None),
    )
    out_specs = P(("node", "dev"), None)
    return jax.shard_map(
        on_device, mesh=mesh, in_specs=in_specs, out_specs=out_specs, check_vma=False
    )
```

profile of v0, /device:TPU:0, one launch (start us, length us, event | category | flops | bytes accessed | tf_op | source)
XLA Modules:
  0.0 85.2 jit_solution(10471312639475334095)
XLA Ops:
  0.0 0.8 reshape.128
  0.8 0.2 convert_reduce_fusion
  1.0 0.8 copy.44
  1.7 0.8 copy.45
  2.6 0.1 copy.46
  2.8 0.1 convolution_convert_fusion.4
  3.0 0.7 copy.47
  3.6 7.3 %all-to-all-start = ((bf16[8,2,4]{2,1,0:T(2,128)(2,1)}), bf16[8,2,4]{2,1,0:T(2,128)(2,1)S(1)}, u32[]{:S(2)}, u32[]{:S(2)}) async-start(bf16[8,2,4]{2,1,0:T(2,128)(2,1)} %bitcast), calls=%async_computation | async-start | bytes 8192 | tf_op jit(solution)/shard_map/all_to_all | solution.py:45
  11.0 0.8 broadcast_in_dim.5
  11.8 0.1 reshape.131
  11.9 0.2 convolution_convert_fusion.3
  12.1 0.7 reshape.132
  12.8 4.6 %all-to-all-done = bf16[8,2,4]{2,1,0:T(2,128)(2,1)S(1)} async-done(((bf16[8,2,4]{2,1,0:T(2,128)(2,1)}), bf16[8,2,4]{2,1,0:T(2,128)(2,1)S(1)}, u32[]{:S(2)}, u32[]{:S(2)}) %all-to-all-start) | async-done | bytes 160 | tf_op jit(solution)/shard_map/all_to_all | solution.py:45
  17.4 3.4 %all-to-all-start.1 = ((bf16[8,2,5120]{2,1,0:T(2,128)(2,1)}), bf16[8,2,5120]{2,1,0:T(2,128)(2,1)S(1)}, u32[]{:S(2)}, u32[]{:S(2)}) async-start(bf16[8,2,5120]{2,1,0:T(2,128)(2,1)} %reshape.132), calls=%async_computation.1 | async-start | bytes 327680 | tf_op jit(solution)/shard_map/all_to_all | solution.py:44
  20.9 0.1 copy.49
  21.3 0.1 fusion.7
  21.5 6.7 %all-to-all-done.1 = bf16[8,2,5120]{2,1,0:T(2,128)(2,1)S(1)} async-done(((bf16[8,2,5120]{2,1,0:T(2,128)(2,1)}), bf16[8,2,5120]{2,1,0:T(2,128)(2,1)S(1)}, u32[]{:S(2)}, u32[]{:S(2)}) %all-to-all-start.1) | async-done | bytes 163872 | tf_op jit(solution)/shard_map/all_to_all | solution.py:44
  28.3 0.3 convolution_convert_fusion.1
  28.7 0.1 reshape_reshape.3
  28.8 12.8 %all_to_all.25 = bf16[4,12,5120]{2,1,0:T(8,128)(2,1)S(1)} all-to-all(bf16[4,12,5120]{2,1,0:T(8,128)(2,1)S(1)} %reshape_reshape.3), channel_id=1, replica_groups=mesh['node'=8,'dev'=4] {'dev'}, dimensions={0} | all-to-all | bytes 983040 | tf_op jit(solution)/shard_map/all_to_all | solution.py:61
  41.6 0.1 reshape.134
  41.7 5.7 %fusion.20 = f32[48,768]{1,0:T(8,128)S(1)} fusion(bf16[48,5120]{1,0:T(8,128)(2,1)S(1)} %reshape.134, bf16[768,5120]{1,0:T(8,128)(2,1)} %param.11), kind=kOutput, calls=%fused_computation.37 | convolution fusion | flops 377487360 | bytes 8503296 | tf_op jit(solution)/shard_map/dot_general | solution.py:65
  47.4 10.3 %convolution_convert_fusion = bf16[48,5120]{1,0:T(8,128)(2,1)S(1)} fusion(bf16[768,5120]{1,0:T(8,128)(2,1)} %param.13, bf16[48,5120]{1,0:T(8,128)(2,1)S(1)} %reshape.134, bf16[768,5120]{1,0:T(8,128)(2,1)} %param.12, f32[48,768]{1,0:T(8,128)S(1)} %fusion.20), kind=kOutput, calls=%fused_computation | convolution fusion | flops 755441664 | bytes 16859136 | tf_op jit(solution)/shard_map/dot_general | solution.py:68
  57.7 0.9 %reshape.135 = bf16[4,12,5120]{2,1,0:T(8,128)(2,1)} reshape(bf16[48,5120]{1,0:T(8,128)(2,1)S(1)} %convolution_convert_fusion) | data formatting | bytes 983040 | tf_op jit(solution)/shard_map/reshape | solution.py:69
  58.6 3.5 %all-to-all-start.3 = ((bf16[4,12,5120]{2,1,0:T(8,128)(2,1)}), bf16[4,12,5120]{2,1,0:T(8,128)(2,1)S(1)}, u32[]{:S(2)}, u32[]{:S(2)}) async-start(bf16[4,12,5120]{2,1,0:T(8,128)(2,1)} %reshape.135), calls=%async_computation.3 | async-start | bytes 1310720 | tf_op jit(solution)/shard_map/all_to_all | solution.py:70
  62.7 9.6 %all-to-all-done.3 = bf16[4,12,5120]{2,1,0:T(8,128)(2,1)S(1)} async-done(((bf16[4,12,5120]{2,1,0:T(8,128)(2,1)}), bf16[4,12,5120]{2,1,0:T(8,128)(2,1)S(1)}, u32[]{:S(2)}, u32[]{:S(2)}) %all-to-all-start.3) | async-done | bytes 491552 | tf_op jit(solution)/shard_map/all_to_all | solution.py:70
  72.3 0.1 reshape.136
  72.4 0.3 convolution_convert_fusion.2
  72.7 0.7 reshape.137
  73.5 3.4 %all-to-all-start.4 = ((bf16[8,2,5120]{2,1,0:T(2,128)(2,1)}), bf16[8,2,5120]{2,1,0:T(2,128)(2,1)S(1)}, u32[]{:S(2)}, u32[]{:S(2)}) async-start(bf16[8,2,5120]{2,1,0:T(2,128)(2,1)} %reshape.137), calls=%async_computation.4 | async-start | bytes 327680 | tf_op jit(solution)/shard_map/all_to_all | solution.py:82
  76.9 7.4 %all-to-all-done.4 = bf16[8,2,5120]{2,1,0:T(2,128)(2,1)S(1)} async-done(((bf16[8,2,5120]{2,1,0:T(2,128)(2,1)}), bf16[8,2,5120]{2,1,0:T(2,128)(2,1)S(1)}, u32[]{:S(2)}, u32[]{:S(2)}) %all-to-all-start.4) | async-done | bytes 163872 | tf_op jit(solution)/shard_map/all_to_all | solution.py:82
  84.4 0.8 convolution_reduce_fusion
  (26 shorter events, 1.5 us)
Async XLA Ops:
  3.6 13.7 %all-to-all-start = ((bf16[8,2,4]{2,1,0:T(2,128)(2,1)}), bf16[8,2,4]{2,1,0:T(2,128)(2,1)S(1)}, u32[]{:S(2)}, u32[]{:S(2)}) async-start(bf16[8,2,4]{2,1,0:T(2,128)(2,1)} %bitcast), calls=%async_computation | async-start | bytes 8192 | tf_op jit(solution)/shard_map/all_to_all | solution.py:45
  17.4 10.9 %all-to-all-start.1 = ((bf16[8,2,5120]{2,1,0:T(2,128)(2,1)}), bf16[8,2,5120]{2,1,0:T(2,128)(2,1)S(1)}, u32[]{:S(2)}, u32[]{:S(2)}) async-start(bf16[8,2,5120]{2,1,0:T(2,128)(2,1)} %reshape.132), calls=%async_computation.1 | async-start | bytes 327680 | tf_op jit(solution)/shard_map/all_to_all | solution.py:44
  58.6 13.7 %all-to-all-start.3 = ((bf16[4,12,5120]{2,1,0:T(8,128)(2,1)}), bf16[4,12,5120]{2,1,0:T(8,128)(2,1)S(1)}, u32[]{:S(2)}, u32[]{:S(2)}) async-start(bf16[4,12,5120]{2,1,0:T(8,128)(2,1)} %reshape.135), calls=%async_computation.3 | async-start | bytes 1310720 | tf_op jit(solution)/shard_map/all_to_all | solution.py:70
  73.5 10.9 %all-to-all-start.4 = ((bf16[8,2,5120]{2,1,0:T(2,128)(2,1)}), bf16[8,2,5120]{2,1,0:T(2,128)(2,1)S(1)}, u32[]{:S(2)}, u32[]{:S(2)}) async-start(bf16[8,2,5120]{2,1,0:T(2,128)(2,1)} %reshape.137), calls=%async_computation.4 | async-start | bytes 327680 | tf_op jit(solution)/shard_map/all_to_all | solution.py:82
where the time goes:
time: 85.8 us; the launch traced here: 85.2 us
  waiting for transfers between devices  28.3 us (33%)
  matrix products  17.7 us (21%)
  starting transfers between devices  17.6 us (21%)
  blocking collectives  12.8 us (15%)
  local copies, waits for them, and re-layouts  8.22 us (10%)
    all_to_all x1, blocking collectives, on_device(): lax.all_to_all(outgoing, 'dev', split_axis=0, concat_axis=0, tiled=True)  12.8 us
    dot_general x1, matrix products, on_device(): jnp.dot(hidden, w_down, preferred_element_type=jnp.float32)  10.3 us
    all_to_all x1, waiting for transfers between devices, on_device(): lax.all_to_all(partial_value, 'dev', split_axis=0, concat_axis=0, tiled=T...  9.58 us
    all_to_all x1, waiting for transfers between devices, on_device(): lax.all_to_all(node_out, 'node', split_axis=0, concat_axis=0, tiled=True)  7.41 us
    all_to_all x1, starting transfers between devices, on_device(): lax.all_to_all(sent_meta, 'node', split_axis=0, concat_axis=0, tiled=True)  7.31 us
    all_to_all x1, waiting for transfers between devices, on_device(): lax.all_to_all(sent_rows, 'node', split_axis=0, concat_axis=0, tiled=True)  6.75 us
    dot_general x1, matrix products, on_device(): lax.dot_general(flat_rows, w_gate, dims, preferred_element_type=jnp.float32)  5.7 us
    all_to_all x1, waiting for transfers between devices, on_device(): lax.all_to_all(sent_meta, 'node', split_axis=0, concat_axis=0, tiled=True)  4.58 us
  transfers between devices with their start and end apart: 4, of which 4 were waited for; matrix products, arithmetic and copies ran while one was open for 4% of the time, Pallas kernels for 0%

commit v1 on v0

--- a/solution.py
+++ b/solution.py
@@ -1,12 +1,16 @@
+import functools
+
 import jax
 import jax.numpy as jnp
 from jax import lax
+from jax.experimental import pallas as pl
+from jax.experimental.pallas import tpu as pltpu
 from jax.sharding import PartitionSpec as P
 
 EXP_NODE = 4
 
 
-def on_device(tokens, node_pick, expert_pick, gate_weight, w_gate, w_up, w_down):
+def plain_form(tokens, node_pick, expert_pick, gate_weight, w_gate, w_up, w_down):
     node_count = lax.axis_size("node")
     dev_count = lax.axis_size("dev")
     tok_rows = tokens.shape[0]
@@ -86,6 +90,324 @@
     return jnp.sum(per_slot.reshape(tok_rows, 3, feature_dim), axis=1).astype(jnp.bfloat16)
 
 
+LANES = 128
+MESH = pl.DeviceIdType.MESH
+CHUNKS = 4
+VMEM_BYTES = 60 * 1024 * 1024
+
+
+def fused_kernel(
+    sizes,
+    tok_ref,
+    node_ref,
+    pick_ref,
+    weight_ref,
+    wg_hbm,
+    wu_hbm,
+    wd_hbm,
+    out_ref,
+    wg,
+    wu,
+    wd,
+    ext,
+    sent,
+    got,
+    stack,
+    rows,
+    gate,
+    up,
+    part_keep,
+    part_out,
+    part_in,
+    node_sent,
+    node_got,
+    home,
+    w_sem,
+    go_send,
+    go_recv,
+    dev_send,
+    dev_recv,
+    red_send,
+    red_recv,
+    back_send,
+    back_recv,
+):
+    nodes, devs, cap, chunks = sizes
+    slots = nodes * cap
+    tok_rows, width = tok_ref.shape
+    step = width // chunks
+    me_n, me_d = lax.axis_index("node"), lax.axis_index("dev")
+    rounds = devs.bit_length() - 1
+    flips = [1 << (rounds - 1 - i) for i in range(rounds)]
+
+    def partner(flip):
+        return me_d + flip * (1 - 2 * (me_d // flip % 2))
+
+    def cols(c, meta=False):
+        return pl.ds(c * step, step + (LANES if meta else 0))
+
+    weight_copies = []
+    for c in range(chunks):
+        for i, (src, dst) in enumerate(((wg_hbm, wg), (wu_hbm, wu))):
+            weight_copies.append(
+                pltpu.make_async_copy(
+                    src.at[:, cols(c)], dst.at[:, cols(c)], w_sem.at[i, c]
+                )
+            )
+    for c in range(chunks):
+        weight_copies.append(
+            pltpu.make_async_copy(
+                wd_hbm.at[:, cols(c)], wd.at[:, cols(c)], w_sem.at[2, c]
+            )
+        )
+    for copy in weight_copies:
+        copy.start()
+
+    barrier = pltpu.get_barrier_semaphore()
+    peers = [(lax.rem(me_n + j, nodes), me_d) for j in range(1, nodes)]
+    peers += [(me_n, partner(flip)) for flip in flips]
+    for peer in peers:
+        pl.semaphore_signal(barrier, inc=1, device_id=peer, device_id_type=MESH)
+
+    lane = lax.broadcasted_iota(jnp.int32, (tok_rows, LANES), 1)
+    down = lax.broadcasted_iota(jnp.int32, (tok_rows, LANES), 0)
+    picked = node_ref[...]
+    hit = jnp.zeros((tok_rows, LANES), jnp.int32)
+    for k in range(3):
+        hit = hit + (picked[:, k : k + 1] == lane // cap).astype(jnp.int32)
+    rank = jnp.zeros((tok_rows, LANES), jnp.int32)
+    for t in range(tok_rows - 1):
+        rank = rank + jnp.where(down > t, hit[t : t + 1, :], 0)
+    table = ((hit > 0) & (rank == lane % cap) & (lane < slots)).astype(jnp.float32)
+    local = pick_ref[...]
+    weights = weight_ref[...].astype(jnp.float32)
+    dense = jnp.zeros((tok_rows, LANES), jnp.float32)
+    for j in range(6):
+        expert = picked[:, j // 2 : j // 2 + 1] * EXP_NODE + local[:, j : j + 1]
+        dense = dense + jnp.where(expert == lane, weights[:, j : j + 1], 0.0)
+    ext[:, :width] = tok_ref[...]
+    ext[:, width:] = dense.astype(jnp.bfloat16)
+    table_t = jnp.transpose(
+        jnp.concatenate([table, jnp.zeros((8 - tok_rows, LANES), jnp.float32)], axis=0)
+    )[:slots, :tok_rows].astype(jnp.bfloat16)
+    placed = jnp.dot(table_t, ext[...], preferred_element_type=jnp.float32)
+    for n in range(nodes):
+        sent[n] = placed[n * cap : (n + 1) * cap].astype(jnp.bfloat16)
+
+    pl.semaphore_wait(barrier, len(peers))
+
+    def node_copy(j, c, source, target, send_sem, recv_sem, where, arriving=False):
+        peer = lax.rem(me_n + j, nodes)
+        landed = lax.rem(me_n + nodes - j, nodes) if arriving else me_n
+        return pltpu.make_async_remote_copy(
+            src_ref=source.at[peer, :, where],
+            dst_ref=target.at[landed, :, where],
+            send_sem=send_sem.at[c, j],
+            recv_sem=recv_sem.at[c, j],
+            device_id=(peer, me_d),
+            device_id_type=MESH,
+        )
+
+    def go(c, j, arriving=False):
+        where = cols(c, c == chunks - 1)
+        return node_copy(j, c, sent, got, go_send, go_recv, where, arriving)
+
+    for c in range(chunks):
+        for j in range(1, nodes):
+            go(c, j).start()
+    got[me_n] = sent[me_n]
+
+    def spread(c, i):
+        held = slots << i
+        where = cols(c, c == chunks - 1)
+        return pltpu.make_async_remote_copy(
+            src_ref=rows.at[pl.ds(0, held), where],
+            dst_ref=rows.at[pl.ds(held, held), where],
+            send_sem=dev_send.at[c, i],
+            recv_sem=dev_recv.at[c, i],
+            device_id=(me_n, partner(flips[i])),
+            device_id_type=MESH,
+        )
+
+    def gather(c, i):
+        if i == 0:
+            where = cols(c, c == chunks - 1)
+            for j in range(1, nodes):
+                go(c, j, True).wait_recv()
+            for n in range(nodes):
+                stack[n * cap : (n + 1) * cap, where] = got[n, :, where].astype(jnp.float32)
+            rows[:slots, where] = stack[:, where].astype(jnp.bfloat16)
+        else:
+            spread(c, i - 1).wait_recv()
+        if i < rounds:
+            spread(c, i).start()
+
+    dims = (((1,), (1,)), ((), ()))
+
+    def project(c):
+        spread(c, rounds - 1).wait_recv()
+        weight_copies[2 * c].wait()
+        weight_copies[2 * c + 1].wait()
+        for acc, w in ((gate, wg), (up, wu)):
+            term = lax.dot_general(
+                rows[:, cols(c)], w[:, cols(c)], dims, preferred_element_type=jnp.float32
+            )
+            acc[...] = term if c == 0 else acc[...] + term
+
+    for wave in range(chunks + rounds):
+        for c in range(chunks):
+            i = wave - c
+            if 0 <= i < rounds:
+                gather(c, i)
+        if wave >= rounds:
+            project(wave - rounds)
+
+    g = gate[...]
+    hidden = (g / (1.0 + jnp.exp(-g)) * up[...]).astype(jnp.bfloat16)
+    total_rows = slots * devs
+    meta = rows[:, width:].astype(jnp.float32)
+    mine = me_n * EXP_NODE + me_d // (devs // EXP_NODE)
+    meta_lane = lax.broadcasted_iota(jnp.int32, (total_rows, LANES), 1)
+    scale = jnp.sum(jnp.where(meta_lane == mine, meta, 0.0), axis=1, keepdims=True)
+
+    def reduce_copy(c, i):
+        half = slots << i
+        return pltpu.make_async_remote_copy(
+            src_ref=part_out.at[pl.ds(half, half), cols(c)],
+            dst_ref=part_in.at[pl.ds(half, half), cols(c)],
+            send_sem=red_send.at[c, i],
+            recv_sem=red_recv.at[c, i],
+            device_id=(me_n, partner(flips[i])),
+            device_id_type=MESH,
+        )
+
+    for c in range(chunks):
+        weight_copies[2 * chunks + c].wait()
+        part = jnp.dot(hidden, wd[:, cols(c)], preferred_element_type=jnp.float32) * scale
+        half = total_rows // 2
+        part_out[half:, cols(c)] = part[half:].astype(jnp.bfloat16)
+        reduce_copy(c, rounds - 1).start()
+        part_keep[:, cols(c)] = part[:half]
+
+    def back(c, j, arriving=False):
+        return node_copy(j, c, node_sent, node_got, back_send, back_recv, cols(c), arriving)
+
+    for i in reversed(range(rounds)):
+        half = slots << i
+        for c in range(chunks):
+            reduce_copy(c, i).wait_recv()
+            total = part_keep[:half, cols(c)] + part_in[
+                half : 2 * half, cols(c)
+            ].astype(jnp.float32)
+            if i > 0:
+                low = half // 2
+                part_out[low:half, cols(c)] = total[low:].astype(jnp.bfloat16)
+                reduce_copy(c, i - 1).start()
+                part_keep[:low, cols(c)] = total[:low]
+            else:
+                for n in range(nodes):
+                    node_sent[n, :, cols(c)] = total[n * cap : (n + 1) * cap].astype(jnp.bfloat16)
+                for j in range(1, nodes):
+                    back(c, j).start()
+                node_got[me_n, :, cols(c)] = node_sent[me_n, :, cols(c)]
+
+    for c in range(chunks):
+        for j in range(1, nodes):
+            back(c, j, True).wait_recv()
+        for n in range(nodes):
+            home[n * cap : (n + 1) * cap, cols(c)] = node_got[n, :, cols(c)].astype(jnp.float32)
+        mixed = jnp.dot(
+            table[:, :slots].astype(jnp.bfloat16),
+            home[:, cols(c)].astype(jnp.bfloat16),
+            preferred_element_type=jnp.float32,
+        )
+        out_ref[:, cols(c)] = mixed.astype(jnp.bfloat16)
+
+    for c in range(chunks):
+        for j in range(1, nodes):
+            go(c, j).wait_send()
+            back(c, j).wait_send()
+        for i in range(rounds):
+            spread(c, i).wait_send()
+            reduce_copy(c, i).wait_send()
+
+
+def fused_form(
+    nodes, devs, cap, tokens, node_pick, expert_pick, gate_weight, w_gate, w_up, w_down
+):
+    tok_rows, width = tokens.shape
+    hidden = w_gate.shape[0]
+    slots = nodes * cap
+    total = slots * devs
+    rounds = devs.bit_length() - 1
+    bf16, f32 = jnp.bfloat16, jnp.float32
+    dma = pltpu.SemaphoreType.DMA
+    scratch = [
+        pltpu.VMEM((hidden, width), bf16),
+        pltpu.VMEM((hidden, width), bf16),
+        pltpu.VMEM((hidden, width), bf16),
+        pltpu.VMEM((tok_rows, width + LANES), bf16),
+        pltpu.VMEM((nodes, cap, width + LANES), bf16),
+        pltpu.VMEM((nodes, cap, width + LANES), bf16),
+        pltpu.VMEM((slots, width + LANES), f32),
+        pltpu.VMEM((total, width + LANES), bf16),
+        pltpu.VMEM((total, hidden), f32),
+        pltpu.VMEM((total, hidden), f32),
+        pltpu.VMEM((total // 2, width), f32),
+        pltpu.VMEM((total, width), bf16),
+        pltpu.VMEM((total, width), bf16),
+        pltpu.VMEM((nodes, cap, width), bf16),
+        pltpu.VMEM((nodes, cap, width), bf16),
+        pltpu.VMEM((slots, width), f32),
+        dma((3, CHUNKS)),
+        dma((CHUNKS, nodes)),
+        dma((CHUNKS, nodes)),
+        dma((CHUNKS, rounds)),
+        dma((CHUNKS, rounds)),
+        dma((CHUNKS, rounds)),
+        dma((CHUNKS, rounds)),
+        dma((CHUNKS, nodes)),
+        dma((CHUNKS, nodes)),
+    ]
+    vmem = pl.BlockSpec(memory_space=pltpu.VMEM)
+    hbm = pl.BlockSpec(memory_space=pl.ANY)
+    return pl.pallas_call(
+        functools.partial(fused_kernel, (nodes, devs, cap, CHUNKS)),
+        out_shape=jax.ShapeDtypeStruct((tok_rows, width), bf16),
+        in_specs=[vmem] * 4 + [hbm] * 3,
+        out_specs=vmem,
+        scratch_shapes=scratch,
+        compiler_params=pltpu.CompilerParams(
+            collective_id=0, has_side_effects=True, vmem_limit_bytes=VMEM_BYTES
+        ),
+    )(tokens, node_pick, expert_pick, gate_weight, w_gate, w_up, w_down)
+
+
+def on_device(*operands):
+    nodes, devs = lax.axis_size("node"), lax.axis_size("dev")
+    tok_rows, width = operands[0].shape
+    hidden = operands[4].shape[0]
+    slot_count = 3 * tok_rows
+    cycle_len = min(nodes, max(3, slot_count // 2))
+    cap = (slot_count + cycle_len - 1) // cycle_len
+    slots = nodes * cap
+    total = slots * devs
+    held = 6 * hidden * width + total * (8 * width + 8 * hidden) + 24 * slots * width
+    fits = (
+        held < VMEM_BYTES * 9 // 10
+        and slots % 16 == 0
+        and slots <= LANES
+        and nodes * EXP_NODE <= LANES
+        and devs & (devs - 1) == 0
+        and devs % EXP_NODE == 0
+        and tok_rows <= 8
+        and width % (CHUNKS * LANES) == 0
+    )
+    if not fits:
+        return plain_form(*operands)
+    return fused_form(nodes, devs, cap, *operands)
+
+
 def solution(mesh):
     in_specs = (
         P(("node", "dev"), None),

time: 85.8 us -> 42.2 us (0.49)
  Pallas kernels: 0 us -> 40.6 us
  waiting for transfers between devices: 28.3 us -> 0 us
  matrix products: 17.7 us -> 0 us
  starting transfers between devices: 17.6 us -> 0 us
  blocking collectives: 12.8 us -> 0 us
  local copies, waits for them, and re-layouts: 8.22 us -> 1.41 us
    pallas_call x0 -> x1, Pallas kernels: none -> 40.6 us  [fused_form(): pl.pallas_call(functools.partial(fused_kernel, (nodes, devs, cap, CHUNKS)...]
    all_to_all x4 -> x0, waiting for transfers between devices: 28.3 us -> none  [the longest x1 9.58 us: on_device(): lax.all_to_all(partial_value, 'dev', split_axis=0, concat_axis=0, tiled=T...]
    dot_general x7 -> x0, matrix products: 17.7 us -> none  [the longest x1 10.3 us: on_device(): jnp.dot(hidden, w_down, preferred_element_type=jnp.float32)]
    all_to_all x4 -> x0, starting transfers between devices: 17.6 us -> none  [the longest x1 7.31 us: on_device(): lax.all_to_all(sent_meta, 'node', split_axis=0, concat_axis=0, tiled=True)]
    all_to_all x1 -> x0, blocking collectives: 12.8 us -> none  [on_device(): lax.all_to_all(outgoing, 'dev', split_axis=0, concat_axis=0, tiled=True)]
    reshape x10 -> x0, local copies, waits for them, and re-layouts: 3.72 us -> none  [the longest x1 0.95 us: on_device(): partial_value = partial_value.reshape(dev_count, item_count, feature_dim)]
    convert_element_type x6 -> x0, local copies, waits for them, and re-layouts: 1.77 us -> none  [the longest x2 0.78 us: on_device(): weights = gate_weight.reshape(tok_rows, 3, 2).astype(jnp.float32)]
    broadcast_in_dim x2 -> x0, local copies, waits for them, and re-layouts: 0.9 us -> none  [the longest x1 0.82 us: on_device(): jnp.repeat(tokens, 3, axis=0)]
  transfers between devices with their start and end apart: 4 -> 0, of which waited for: 4 -> 0; matrix products, arithmetic and copies ran while one was open for 4% -> 0% of each run, Pallas kernels for 0% -> 0%
where the time goes in v1:
time: 42.2 us; the launch traced here: 42 us
  Pallas kernels  40.6 us (96%)
  local copies, waits for them, and re-layouts  1.41 us (3%)
    pallas_call x1, Pallas kernels, fused_form(): pl.pallas_call(functools.partial(fused_kernel, (nodes, devs, cap, CHUNKS)...  40.6 us
    unnamed x1, local copies, waits for them, and re-layouts  1.41 us

profile of v1, /device:TPU:0, one launch (start us, length us, event | category | flops | bytes accessed | tf_op | source)
XLA Modules:
  0.0 42.0 jit_solution(16339268581977132833)
XLA Ops:
  0.0 40.6 %shard_map.73 = bf16[4,5120]{1,0:T(4,128)(2,1)} custom-call(bf16[4,5120]{1,0:T(4,128)(2,1)} %tok_ref.1, s32[4,3]{1,0:T(4,128)} %node_ref.1, s32[4,6]{1,0:T(4,128)} %pick_ref.1, bf16[4,6]{1,0:T(4,128)(2,1)} %weight_ref.1, bf16[768,5120]{1,0:T(8,128)(2,1)} %wg_hbm.1, bf16[768,5120]{1,0:T(8,128)(2,1)} %wu_hbm.1, bf16[768,5120]{1,0:T(8,128)(2,1)} %wd_hbm.1), custom_call_target="tpu_custom_call" | custom-call | tf_op jit(solution)/shard_map/pallas_call | solution.py:374
  40.6 1.4 %copy.9 = bf16[4,5120]{1,0:T(4,128)(2,1)} copy(bf16[4,5120]{1,0:T(4,128)(2,1)} %shard_map.73) | data formatting | bytes 81920

commit v2 on v1

--- a/solution.py
+++ b/solution.py
@@ -92,7 +92,7 @@
 
 LANES = 128
 MESH = pl.DeviceIdType.MESH
-CHUNKS = 4
+CHUNKS = 1
 VMEM_BYTES = 60 * 1024 * 1024
 
 

time: 42.2 us -> 37.5 us (0.89)
  Pallas kernels: 40.6 us -> 35.9 us
    pallas_call x1, Pallas kernels: 40.6 us -> 35.9 us  [fused_form(): pl.pallas_call(functools.partial(fused_kernel, (nodes, devs, cap, CHUNKS)...]
where the time goes in v2:
time: 37.5 us; the launch traced here: 37.3 us
  Pallas kernels  35.9 us (96%)
  local copies, waits for them, and re-layouts  1.41 us (4%)
    pallas_call x1, Pallas kernels, fused_form(): pl.pallas_call(functools.partial(fused_kernel, (nodes, devs, cap, CHUNKS)...  35.9 us
    unnamed x1, local copies, waits for them, and re-layouts  1.41 us

profile of v2, /device:TPU:0, one launch (start us, length us, event | category | flops | bytes accessed | tf_op | source)
XLA Modules:
  0.0 37.3 jit_solution(2262690694312469232)
XLA Ops:
  0.0 35.9 %shard_map.73 = bf16[4,5120]{1,0:T(4,128)(2,1)} custom-call(bf16[4,5120]{1,0:T(4,128)(2,1)} %tok_ref.1, s32[4,3]{1,0:T(4,128)} %node_ref.1, s32[4,6]{1,0:T(4,128)} %pick_ref.1, bf16[4,6]{1,0:T(4,128)(2,1)} %weight_ref.1, bf16[768,5120]{1,0:T(8,128)(2,1)} %wg_hbm.1, bf16[768,5120]{1,0:T(8,128)(2,1)} %wu_hbm.1, bf16[768,5120]{1,0:T(8,128)(2,1)} %wd_hbm.1), custom_call_target="tpu_custom_call" | custom-call | tf_op jit(solution)/shard_map/pallas_call | solution.py:374
  35.9 1.4 %copy.9 = bf16[4,5120]{1,0:T(4,128)(2,1)} copy(bf16[4,5120]{1,0:T(4,128)(2,1)} %shard_map.73) | data formatting | bytes 81920
